TPU v7x, 32 devices: a whole 2x2x4 slice. The times are simulated.
32 devices in a mesh: group: 8 (over z, y), local: 4 (over x, core).
Axes of the slice: x: 2, y: 2, z: 4, core: 2. Of those that a mesh axis runs over, the one named last changes fastest.
Arguments:
- dense_vec: bfloat16 [4096, 128], P(('group', 'local')), may hold values from -6 to 6
- q_tables: float32 [1024, 26, 128], P('group'), may hold values from -4 to 4
- r_tables: float32 [256, 26, 128], P('local'), may hold values from -4 to 4
- owner: int32 [4096, 26, 1], P(('group', 'local')), may hold values from 0 to 7; in each aligned block of 3328 rows (0 to 3327, 3328 to 6655, ..., all dimensions but the last counted through in order) at most 832 rows name the same one
- q_local: int32 [4096, 26], P(('group', 'local')), may hold values from 0 to 127
- r_index: int32 [4096, 26], P(('group', 'local')), may hold values from 0 to 255
- w_one: bfloat16 [479, 1024], replicated, may hold values from -0.25 to 0.25
- b_one: float32 [1024], replicated, may hold values from -3 to 3
- w_two: bfloat16 [1024, 1024], replicated, may hold values from -0.1875 to 0.1875
- b_two: float32 [1024], replicated, may hold values from -3 to 3
- w_three: bfloat16 [1024, 512], replicated, may hold values from -0.1875 to 0.1875
- b_three: float32 [512], replicated, may hold values from -3 to 3
- w_four: bfloat16 [512, 256], replicated, may hold values from -0.25 to 0.25
- b_four: float32 [256], replicated, may hold values from -3 to 3
- cotangent: bfloat16 [4096, 256], P(('group', 'local')), may hold values from -6 to 6
Outputs:
- q_new: float32 [1024, 26, 128], P('group')
- r_new: float32 [256, 26, 128], P('local')
- w_one_new: float32 [479, 1024], replicated
- b_one_new: float32 [1024], replicated
- w_two_new: float32 [1024, 1024], replicated
- b_two_new: float32 [1024], replicated
- w_three_new: float32 [1024, 512], replicated
- b_three_new: float32 [512], replicated
- w_four_new: float32 [512, 256], replicated
- b_four_new: float32 [256], replicated
Inputs may be any that keep to these rules, and one draw needn't show every extreme that they name: `owner`: within the rows of one device (its 128 samples times 26 tables), no group is named more than 832 times, a bound that some block reaches.
All inputs are finite; a program needn't handle non-finite values.
Results may differ from a plain program's by a relative error of at most 0.0025.
Values may be sent and summed in bfloat16 or wider, within the bound.
A program may use at most 128 MiB of HBM per device.

v0:
```python
import jax
import jax.numpy as jnp
import numpy as np
from jax import lax
from jax.sharding import PartitionSpec as P

table_rate = 0.05
dense_rate = 0.0005


def silu_slope(preact):
    sigma = jax.nn.sigmoid(preact)
    return sigma * (1.0 + preact * (1.0 - sigma))


def interact(dense_rows, embeds):
    vectors_all = jnp.concatenate([dense_rows[:, None, :], embeds], axis=1).astype(jnp.float32)
    gram_mat = jnp.einsum("bid,bjd->bij", vectors_all, vectors_all, precision=lax.Precision.HIGHEST)
    lower_i, lower_j = np.tril_indices(vectors_all.shape[1], -1)
    pair_vals = gram_mat[:, lower_i, lower_j]
    features = jnp.concatenate([dense_rows.astype(jnp.float32), pair_vals], axis=1).astype(
        jnp.bfloat16
    )
    return (vectors_all, features)


def pair_back(d_pairs, vectors_all):
    vectors = vectors_all.shape[1]
    lower_i, lower_j = np.tril_indices(vectors, -1)
    spread = (
        jnp.zeros((vectors_all.shape[0], vectors, vectors), jnp.float32)
        .at[:, lower_i, lower_j]
        .set(d_pairs)
    )
    spread = spread + jnp.swapaxes(spread, 1, 2)
    return jnp.einsum("bij,bjd->bid", spread, vectors_all, precision=lax.Precision.HIGHEST)


def contract_rows(left, right):
    return lax.dot_general(
        left, right, (((0,), (0,)), ((), ())), preferred_element_type=jnp.float32
    )


def dense_pass(features, layers, cot_rows):
    inputs_list = [features]
    pre_list = []
    current = features
    for layer_idx, (weight, biases) in enumerate(layers):
        pre_act = jnp.dot(current, weight, preferred_element_type=jnp.float32) + biases
        pre_list.append(pre_act)
        if layer_idx + 1 < len(layers):
            current = jax.nn.silu(pre_act).astype(jnp.bfloat16)
            inputs_list.append(current)
    grad_low = cot_rows
    grad_full = cot_rows.astype(jnp.float32)
    grads = []
    back_grad = None
    for layer_idx in reversed(range(len(layers))):
        weight = layers[layer_idx][0]
        w_grad = contract_rows(inputs_list[layer_idx], grad_low)
        b_grad = jnp.sum(grad_full, axis=0)
        back_grad = lax.dot_general(
            grad_low, weight, (((1,), (1,)), ((), ())), preferred_element_type=jnp.float32
        )
        grads.insert(0, (w_grad, b_grad))
        if layer_idx > 0:
            grad_full = back_grad * silu_slope(pre_list[layer_idx - 1])
            grad_low = grad_full.astype(jnp.bfloat16)
    return (grads, back_grad)


def body(
    dense_vec,
    q_tables,
    r_tables,
    owner,
    q_local,
    r_index,
    w_one,
    b_one,
    w_two,
    b_two,
    w_three,
    b_three,
    w_four,
    b_four,
    cotangent,
):
    layers = [(w_one, b_one), (w_two, b_two), (w_three, b_three), (w_four, b_four)]
    groups = lax.axis_size("group")
    batch_rows, table_count = q_local.shape
    embed_width = q_tables.shape[2]
    lookups = batch_rows * table_count
    capacity = 2 * lookups // groups
    slot_count = groups * capacity
    segment_count = q_tables.shape[0] * table_count
    table_ids = jnp.arange(table_count, dtype=jnp.int32)[None, :]
    highest = lax.Precision.HIGHEST
    dest_group = owner[:, :, 0]
    owner_hits = (
        dest_group[:, :, None] == jnp.arange(groups, dtype=jnp.int32)[None, None, :]
    ).astype(jnp.float32)
    table_lower = (jnp.arange(table_count)[:, None] < jnp.arange(table_count)[None, :]).astype(
        jnp.float32
    )
    sample_lower = (jnp.arange(batch_rows)[:, None] < jnp.arange(batch_rows)[None, :]).astype(
        jnp.float32
    )
    within = jnp.einsum("st,bsg->btg", table_lower, owner_hits, precision=highest)
    before = jnp.einsum("cb,cg->bg", sample_lower, jnp.sum(owner_hits, axis=1), precision=highest)
    slot_rank = jnp.sum((within + before[:, None, :]) * owner_hits, axis=2).astype(jnp.int32)
    position = (dest_group * capacity + slot_rank).reshape(lookups)
    source = (
        jnp.full((slot_count,), lookups, jnp.int32)
        .at[position]
        .set(jnp.arange(lookups, dtype=jnp.int32))
    )
    row_keys = (q_local * table_count + table_ids).reshape(lookups)
    keys_padded = jnp.concatenate([row_keys, jnp.zeros((1,), jnp.int32)])
    outgoing = keys_padded[source].reshape(groups, capacity)
    flat_table = q_tables.reshape(segment_count, embed_width)
    request = lax.all_to_all(outgoing, "group", split_axis=0, concat_axis=0, tiled=True)
    served_rows = flat_table[request].astype(jnp.bfloat16)
    arrived = lax.all_to_all(served_rows, "group", split_axis=0, concat_axis=0, tiled=True)
    q_rows = arrived.reshape(slot_count, embed_width)[position]
    full_r = lax.all_gather(r_tables, "local", axis=0, tiled=True)
    remainder_count = full_r.shape[0]
    r_pick = (
        r_index[:, :, None] == jnp.arange(remainder_count, dtype=jnp.int32)[None, None, :]
    ).astype(jnp.float32)
    r_rows = jnp.einsum("btr,rtd->btd", r_pick, full_r, precision=highest).reshape(
        lookups, embed_width
    )
    q_val = q_rows.astype(jnp.float32)
    embeds = (q_val * r_rows).astype(jnp.bfloat16).reshape(batch_rows, table_count, embed_width)
    vectors_all, features = interact(dense_vec, embeds)
    grads, d_features = dense_pass(features, layers, cotangent)
    d_embed = pair_back(d_features[:, embed_width:], vectors_all)[:, 1:, :].reshape(
        lookups, embed_width
    )
    grad_padded = jnp.concatenate(
        [d_embed * r_rows, jnp.zeros((1, embed_width), jnp.float32)], axis=0
    )
    outbound = grad_padded[source].reshape(groups, capacity, embed_width)
    returned = (
        lax.all_to_all(
            outbound.astype(jnp.bfloat16), "group", split_axis=0, concat_axis=0, tiled=True
        )
        .astype(outbound.dtype)
        .reshape(slot_count, embed_width)
    )
    served_flat = request.reshape(slot_count)
    q_part = jax.ops.segment_sum(returned, served_flat, num_segments=segment_count).reshape(
        q_tables.shape
    )
    q_piece = lax.psum_scatter(
        q_part.astype(jnp.bfloat16), "local", scatter_dimension=0, tiled=True
    ).astype(jnp.float32)
    quarter = q_piece.shape[0]
    own_rows = lax.dynamic_slice_in_dim(q_tables, lax.axis_index("local") * quarter, quarter, 0)
    q_new = lax.all_gather(own_rows - table_rate * q_piece, "local", axis=0, tiled=True)
    r_part = jnp.einsum(
        "btr,btd->rtd",
        r_pick,
        (d_embed * q_val).reshape(batch_rows, table_count, embed_width),
        precision=highest,
    )
    summed = lax.psum(r_part, ("group", "local"))
    r_grad = lax.dynamic_slice_in_dim(
        summed, lax.axis_index("local") * r_tables.shape[0], r_tables.shape[0], 0
    )
    r_new = r_tables - table_rate * r_grad
    grad_wa, grad_ba, grad_wb, grad_bb, grad_wc, grad_bc, grad_wd, grad_bd = lax.psum(
        (
            grads[0][0],
            grads[0][1],
            grads[1][0],
            grads[1][1],
            grads[2][0],
            grads[2][1],
            grads[3][0],
            grads[3][1],
        ),
        ("group", "local"),
    )
    summed_grads = [(grad_wa, grad_ba), (grad_wb, grad_bb), (grad_wc, grad_bc), (grad_wd, grad_bd)]
    updated = []
    for (weight, biases), (w_grad, b_grad) in zip(layers, summed_grads):
        updated.append(weight.astype(jnp.float32) - dense_rate * w_grad)
        updated.append(biases - dense_rate * b_grad)
    return (
        q_new,
        r_new,
        updated[0],
        updated[1],
        updated[2],
        updated[3],
        updated[4],
        updated[5],
        updated[6],
        updated[7],
    )


def solution(mesh):
    return jax.shard_map(
        body,
        mesh=mesh,
        in_specs=(
            P(("group", "local"), None),
            P("group", None, None),
            P("local", None, None),
            P(("group", "local"), None, None),
            P(("group", "local"), None),
            P(("group", "local"), None),
            P(),
            P(),
            P(),
            P(),
            P(),
            P(),
            P(),
            P(),
            P(("group", "local"), None),
        ),
        out_specs=(
            P("group", None, None),
            P("local", None, None),
            P(),
            P(),
            P(),
            P(),
            P(),
            P(),
            P(),
            P(),
        ),
        check_vma=False,
    )
```

profile of v0, /device:TPU:0, one launch (start us, length us, event | category | flops | bytes accessed | tf_op | source)
XLA Modules:
  0.0 590.5 jit_solution(14401636984354006459)
XLA Ops:
  11.3 12.8 %scatter_custom_fusion = s32[6656]{0:T(1024)S(1)} fusion(s32[3328]{0:T(1024)S(1)} %fusion.38, s32[3328]{0:T(1024)S(1)} %iota.29, s32[]{:T(128)} %constant.27.clone.1), kind=kCustom, calls=%fused_computation.84 | custom fusion | bytes 26628 | tf_op jit(solution)/shard_map/scatter | solution.py:117
  24.1 34.5 %gather_fusion = s32[6656]{0:T(1024)S(1)} fusion(s32[3329]{0:T(1024)S(1)} %pad_add_fusion, s32[7168]{0:T(1024)S(1)} %pad_clamp_fusion.1), kind=kCustom, calls=%fused_computation | custom fusion | bytes 79872 | tf_op jit(solution)/shard_map/gather | solution.py:121
  59.4 7.3 %all-to-all-start = ((s32[8,1,832]{2,1,0:T(1,128)}), s32[8,1,832]{2,1,0:T(1,128)S(1)}, u32[]{:S(2)}, u32[]{:S(2)}) async-start(s32[8,1,832]{2,1,0:T(1,128)} %all_to_all.14), calls=%async_computation | async-start | bytes 57344 | tf_op jit(solution)/shard_map/all_to_all | solution.py:123
  69.4 4.0 all-to-all-done
  73.5 14.3 %gather_fusion.1 = bf16[6656,128]{1,0:T(8,128)(2,1)} fusion(bf16[3328,128]{1,0:T(8,128)(2,1)S(1)} %reshape.127, s32[7168]{0:T(1024)S(1)} %pad_clamp_fusion), kind=kCustom, calls=%fused_computation.1 | custom fusion | bytes 3434496 | tf_op jit(solution)/shard_map/gather | solution.py:124
  87.8 3.8 all-to-all-start.1
  91.7 38.3 %all-to-all-done.1 = bf16[8,832,128]{2,1,0:T(8,128)(2,1)S(1)} async-done(((bf16[8,832,128]{2,1,0:T(8,128)(2,1)}), bf16[8,832,128]{2,1,0:T(8,128)(2,1)S(1)}, u32[]{:S(2)}, u32[]{:S(2)}) %all-to-all-start.1) | async-done | bytes 1703968 | tf_op jit(solution)/shard_map/all_to_all | solution.py:125
  130.0 6.5 %gather_fusion.2 = bf16[3328,128]{1,0:T(8,128)(2,1)S(1)} fusion(bf16[6656,128]{1,0:T(8,128)(2,1)S(1)} %bitcast.53, s32[4096]{0:T(1024)S(1)} %pad_clamp_fusion.2), kind=kCustom, calls=%fused_computation.2 | custom fusion | bytes 1717248 | tf_op jit(solution)/shard_map/gather | solution.py:126
  137.2 7.3 %fusion.5 = (bf16[128,26,128]{2,0,1:T(8,128)(2,1)S(1)}, f32[26,128,128]{2,1,0:T(8,128)}) fusion(f32[128,26,128]{2,1,0:T(8,128)S(1)} %reshape.131, f32[256,26,128]{2,0,1:T(8,128)} %all-gather.3.cloned.1.call-done, s32[128,26]{0,1:T(8,128)S(1)} %copy-done.28), kind=kOutput, calls=%fused_computation.19 | convolution fusion | flops 1310326784 | bytes 7681024 | tf_op jit(solution)/shard_map/btr,rtd->btd/dot_general | solution.py:132
  146.4 4.9 gather_fusion.3
  160.7 19.0 %scatter_fusion = f32[128,27,27]{0,2,1:T(8,128)S(1)} fusion(f32[128,27,27]{0,2,1:T(8,128)S(1)} %broadcast_in_dim.21, s32[351]{0:T(512)S(1)} %copy-done, f32[351,128]{1,0:T(8,128)S(1)} %convolution_bitcast_fusion), kind=kCustom, calls=%fused_computation.6 | custom fusion | bytes 541944 | tf_op jit(solution)/shard_map/scatter | solution.py:33
  180.0 2.9 copy.87
  182.9 3.3 fusion.14
  190.2 15.5 %gather_fusion.4 = bf16[6656,128]{1,0:T(8,128)(2,1)} fusion(bf16[3329,128]{1,0:T(8,128)(2,1)S(1)} %concatenate.24, s32[7168]{0:T(1024)} %copy-done.22), kind=kCustom, calls=%fused_computation.4 | custom fusion | bytes 3434496 | tf_op jit(solution)/shard_map/gather | solution.py:145
  205.7 4.4 all-to-all-start.2
  210.3 39.2 %all-to-all-done.2 = bf16[8,832,128]{2,1,0:T(8,128)(2,1)} async-done(((bf16[8,832,128]{2,1,0:T(8,128)(2,1)}), bf16[8,832,128]{2,1,0:T(8,128)(2,1)}, u32[]{:S(2)}, u32[]{:S(2)}) %all-to-all-start.2) | async-done | bytes 1703968 | tf_op jit(solution)/shard_map/all_to_all | solution.py:147
  249.5 40.3 %scatter_custom_fusion.2 = f32[3328,128]{1,0:T(8,128)} fusion(s32[6656]{0:T(1024)S(1)} %reshape.188, bf16[6656,128]{1,0:T(8,128)(2,1)} %bitcast.13, f32[]{:T(128)} %constant.24.clone.1), kind=kCustom, calls=%fused_computation.9 | custom fusion | flops 1703936 | bytes 3407876 | tf_op jit(solution)/shard_map/scatter-add | solution.py:154
  301.1 6.2 %fusion.4 = f32[256,26,128]{0,2,1:T(8,128)} fusion(s32[128,26]{0,1:T(8,128)S(1)} %copy-done.28, f32[128,26,128]{2,1,0:T(8,128)S(1)} %fusion.14, f32[128,26,128]{2,1,0:T(8,128)S(1)} %copy-done.2), kind=kOutput, calls=%fused_computation.16 | convolution fusion | flops 1309900800 | bytes 6829056 | tf_op jit(solution)/shard_map/btr,btd->rtd/dot_general | solution.py:163
  307.3 14.6 %reduce-scatter.2.cloned.1.call-done = bf16[32,26,128]{2,1,0:T(8,128)(2,1)} async-done(((bf16[128,26,128]{2,1,0:T(8,128)(2,1)}), bf16[32,26,128]{2,1,0:T(8,128)(2,1)}) %reduce-scatter.2.cloned.1.call-update) | async-done | bytes 213008 | tf_op jit(solution)/shard_map/reduce_scatter | solution.py:157
  324.8 40.8 %all-reduce.1 = (f32[1024]{0:T(1024)S(1)}, f32[1024]{0:T(1024)S(1)}, f32[512]{0:T(512)S(1)}, f32[256]{0:T(256)S(1)}) all-reduce(f32[1024]{0:T(1024)S(1)} %copy-done.34, f32[1024]{0:T(1024)S(1)} %copy-done.33, f32[512]{0:T(512)S(1)} %copy-done.37, f32[256]{0:T(256)S(1)} %convert_reduce_fusion), channel_id=1, replica_groups=mesh['group'=8,'local'=4] {'group','local'}, use_global_device_ids=true, to_apply=%region_9.10 | all-reduce | flops 2816 | bytes 22528 | tf_op jit(solution)/shard_map/psum | solution.py:174
  367.4 192.2 %all-reduce.5.cloned.1.call-done = (f32[256,26,128]{0,2,1:T(8,128)}, f32[479,1024]{1,0:T(8,128)}, f32[1024,1024]{1,0:T(8,128)}, f32[1024,512]{1,0:T(8,128)}, f32[512,256]{1,0:T(8,128)}) async-done(((f32[256,26,128]{0,2,1:T(8,128)}, f32[479,1024]{1,0:T(8,128)}, f32[1024,1024]{1,0:T(8,128)}, f32[1024,512]{1,0:T(8,128)}, f32[512,256]{1,0:T(8,128)}), (f32[256,26,128]{0,2,1:T(8,128)}, f32[479,1024]{1,0:T(8,128)}, ...) | async-done | bytes 12185616 | tf_op jit(solution)/shard_map/psum | solution.py:169
  564.8 3.4 multiply_subtract_fusion.2
  574.0 7.2 %all-gather.5.cloned.1.call-done = f32[128,26,128]{2,0,1:T(8,128)} async-done(((f32[32,26,128]{2,0,1:T(8,128)}), f32[128,26,128]{2,0,1:T(8,128)}) %all-gather.5.cloned.1.call-update) | async-done | bytes 1703952 | tf_op jit(solution)/shard_map/all_gather | solution.py:162
  581.2 2.8 copy.112
  (153 shorter events, 50.8 us)
Async XLA Ops:
  7.2 129.6 %all-gather.3.cloned.1.call-start = ((), (), s32[]{:S(2)}) async-start(), calls=%async_computation.4 | async-start | bytes 4259840 | tf_op jit(solution)/shard_map/all_gather | solution.py:127
  24.1 34.6 %copy-start.22 = (s32[7168]{0:T(1024)}, s32[7168]{0:T(1024)S(1)}, u32[]{:S(2)}) copy-start(s32[7168]{0:T(1024)S(1)} %pad_clamp_fusion.1) | copy-start | bytes 86020
  59.4 14.0 %all-to-all-start = ((s32[8,1,832]{2,1,0:T(1,128)}), s32[8,1,832]{2,1,0:T(1,128)S(1)}, u32[]{:S(2)}, u32[]{:S(2)}) async-start(s32[8,1,832]{2,1,0:T(1,128)} %all_to_all.14), calls=%async_computation | async-start | bytes 57344 | tf_op jit(solution)/shard_map/all_to_all | solution.py:123
  69.1 18.6 %copy-start.3 = (f32[128,26,128]{2,1,0:T(8,128)}, f32[128,26,128]{2,1,0:T(8,128)S(1)}, u32[]{:S(2)}) copy-start(f32[128,26,128]{2,1,0:T(8,128)S(1)} %copy.64) | copy-start | bytes 5111812
  73.3 14.4 %copy-start.23 = (s32[8,1,832]{2,1,0:T(1,128)}, s32[8,1,832]{2,1,0:T(1,128)S(1)}, u32[]{:S(2)}) copy-start(s32[8,1,832]{2,1,0:T(1,128)S(1)} %all-to-all-done) | copy-start | bytes 79876
  87.8 3.8 copy-start.25
  87.8 42.2 %all-to-all-start.1 = ((bf16[8,832,128]{2,1,0:T(8,128)(2,1)}), bf16[8,832,128]{2,1,0:T(8,128)(2,1)S(1)}, u32[]{:S(2)}, u32[]{:S(2)}) async-start(bf16[8,832,128]{2,1,0:T(8,128)(2,1)} %bitcast.55), calls=%async_computation.1 | async-start | bytes 3407872 | tf_op jit(solution)/shard_map/all_to_all | solution.py:125
  136.7 7.8 %copy-start.1 = (f32[128,26,128]{2,1,0:T(8,128)}, f32[128,26,128]{2,1,0:T(8,128)S(1)}, u32[]{:S(2)}) copy-start(f32[128,26,128]{2,1,0:T(8,128)S(1)} %reshape.131) | copy-start | bytes 5111812
  144.6 6.7 %copy-start.31 = (f32[1024]{0:T(1024)S(1)}, f32[1024]{0:T(1024)}, u32[]{:S(2)}) copy-start(f32[1024]{0:T(1024)} %param.30) | copy-start | bytes 12292
  145.3 7.6 %copy-start.32 = (f32[1024]{0:T(1024)S(1)}, f32[1024]{0:T(1024)}, u32[]{:S(2)}) copy-start(f32[1024]{0:T(1024)} %param.32) | copy-start | bytes 12292
  152.8 5.4 copy-start.11
  160.3 19.4 %copy-start.20 = (bf16[128,1024]{1,0:T(8,128)(2,1)}, bf16[128,1024]{1,0:T(8,128)(2,1)S(1)}, u32[]{:S(2)}) copy-start(bf16[128,1024]{1,0:T(8,128)(2,1)S(1)} %get-tuple-element.52) | copy-start | bytes 786436
  205.7 4.5 copy-start.24
  205.7 43.8 %all-to-all-start.2 = ((bf16[8,832,128]{2,1,0:T(8,128)(2,1)}), bf16[8,832,128]{2,1,0:T(8,128)(2,1)}, u32[]{:S(2)}, u32[]{:S(2)}) async-start(bf16[8,832,128]{2,1,0:T(8,128)(2,1)} %bitcast.54), calls=%async_computation.2 | async-start | bytes 3407872 | tf_op jit(solution)/shard_map/all_to_all | solution.py:147
  210.1 111.8 %reduce-scatter.2.cloned.1.call-start = ((), (), s32[]{:S(2)}) async-start(), calls=%async_computation.5 | async-start | bytes 1310720 | tf_op jit(solution)/shard_map/reduce_scatter | solution.py:157
  292.6 3.9 copy-start.18
  292.6 3.9 copy-start.27
  292.6 266.9 %all-reduce.5.cloned.1.call-start = ((), (), s32[]{:S(2)}) async-start(), calls=%async_computation.7 | async-start | bytes 24379392 | tf_op jit(solution)/shard_map/psum | solution.py:169
  307.3 16.9 %copy-start.8 = (f32[64,26,128]{2,0,1:T(8,128)S(1)}, f32[64,26,128]{2,0,1:T(8,128)}, u32[]{:S(2)}) copy-start(f32[64,26,128]{2,0,1:T(8,128)} %param.25) | copy-start | bytes 2555908
  307.3 273.9 %all-gather.5.cloned.1.call-start = ((), (), s32[]{:S(2)}) async-start(), calls=%async_computation.6 | async-start | bytes 2129920 | tf_op jit(solution)/shard_map/all_gather | solution.py:162
  323.1 42.5 %copy-start.38 = (f32[256]{0:T(256)S(1)}, f32[256]{0:T(256)}, u32[]{:S(2)}) copy-start(f32[256]{0:T(256)} %param.36) | copy-start | bytes 3076
  323.2 43.0 %copy-start.36 = (f32[512]{0:T(512)S(1)}, f32[512]{0:T(512)}, u32[]{:S(2)}) copy-start(f32[512]{0:T(512)} %param.34) | copy-start | bytes 6148
  562.9 5.3 copy-start.15
  564.8 5.1 copy-start.10
  (23 other events, 48.7 us)
Sparse Core Ops, SparseCore 0:
  9.5 32.7 all-gather.2
  292.7 29.1 reduce-scatter.1
  328.9 230.5 all-reduce.4
  561.5 19.5 all-gather.4
where the time goes:
time: 592 us; the launch traced here: 591 us
  waiting for transfers between devices  296 us (50%)
  local copies, waits for them, and re-layouts  130 us (22%)
  other arithmetic  59.6 us (10%)
  blocking collectives  40.8 us (7%)
  matrix products  34 us (6%)
  starting transfers between devices  15.7 us (3%)
  between operations  14.4 us (2%)
    psum x1, waiting for transfers between devices, body(): summed = lax.psum(r_part, ('group', 'local'))  192 us
    psum x1, blocking collectives, body(): lax.psum((grads[0][0], grads[0][1], grads[1][0], grads[1][1], grads[2][0]...  40.8 us
    scatter-add x1, other arithmetic, body(): jax.ops.segment_sum(returned, served_flat, num_segments=segment_count)  40.3 us
    all_to_all x1, waiting for transfers between devices, body(): lax.all_to_all(outbound.astype(jnp.bfloat16), 'group', split_axis=0, conc...  39.2 us
    all_to_all x1, waiting for transfers between devices, body(): lax.all_to_all(served_rows, 'group', split_axis=0, concat_axis=0, tiled=T...  38.3 us
    gather x1, local copies, waits for them, and re-layouts, body(): outgoing = keys_padded[source].reshape(groups, capacity)  34.5 us
    scatter x1, local copies, waits for them, and re-layouts, pair_back(): spread = jnp.zeros((vectors_all.shape[0], vectors, vectors), jnp.float32)...  19 us
    gather x1, local copies, waits for them, and re-layouts, body(): outbound = grad_padded[source].reshape(groups, capacity, embed_width)  15.5 us
  transfers between devices with their start and end apart: 7, of which 6 were waited for; matrix products, arithmetic and copies ran while one was open for 18% of the time, Pallas kernels for 0%

commit v1 on v0

--- a/solution.py
+++ b/solution.py
@@ -166,7 +166,7 @@
         (d_embed * q_val).reshape(batch_rows, table_count, embed_width),
         precision=highest,
     )
-    summed = lax.psum(r_part, ("group", "local"))
+    summed = lax.psum(lax.psum(r_part, "group"), "local")
     r_grad = lax.dynamic_slice_in_dim(
         summed, lax.axis_index("local") * r_tables.shape[0], r_tables.shape[0], 0
     )

time: 592 us -> 681 us (1.15)
  waiting for transfers between devices: 296 us -> 389 us
    psum x1 -> x3, waiting for transfers between devices: 192 us -> 241 us  [the longest x1 144 us: body(): lax.psum((grads[0][0], grads[0][1], grads[1][0], grads[1][1], grads[2][0]...]
    all_to_all x1, waiting for transfers between devices: 39.2 us -> 58.9 us  [body(): lax.all_to_all(outbound.astype(jnp.bfloat16), 'group', split_axis=0, conc...]
    reduce_scatter x1, waiting for transfers between devices: 14.6 us -> 26.9 us  [body(): lax.psum_scatter(q_part.astype(jnp.bfloat16), 'local', scatter_dimension=...]
    all_gather x1, waiting for transfers between devices: 7.17 us -> 19.2 us  [body(): lax.all_gather(own_rows - table_rate * q_piece, 'local', axis=0, tiled=True)]
    unnamed x87 -> x73, local copies, waits for them, and re-layouts: 14.2 us -> 15.2 us
  transfers between devices with their start and end apart: 7 -> 9, of which waited for: 6 -> 8; matrix products, arithmetic and copies ran while one was open for 18% -> 24% of each run, Pallas kernels for 0% -> 0%
where the time goes in v1:
time: 681 us; the launch traced here: 680 us
  waiting for transfers between devices  389 us (57%)
  local copies, waits for them, and re-layouts  128 us (19%)
  other arithmetic  60.9 us (9%)
  blocking collectives  41.1 us (6%)
  matrix products  30.6 us (4%)
  starting transfers between devices  15.3 us (2%)
  between operations  14.8 us (2%)
    psum x1, waiting for transfers between devices, body(): lax.psum((grads[0][0], grads[0][1], grads[1][0], grads[1][1], grads[2][0]...  144 us
    psum x2, waiting for transfers between devices, body(): summed = lax.psum(lax.psum(r_part, 'group'), 'local')  96.9 us
    all_to_all x1, waiting for transfers between devices, body(): lax.all_to_all(outbound.astype(jnp.bfloat16), 'group', split_axis=0, conc...  58.9 us
    psum x1, blocking collectives, body(): lax.psum((grads[0][0], grads[0][1], grads[1][0], grads[1][1], grads[2][0]...  41.1 us
    scatter-add x1, other arithmetic, body(): jax.ops.segment_sum(returned, served_flat, num_segments=segment_count)  39.3 us
    all_to_all x1, waiting for transfers between devices, body(): lax.all_to_all(served_rows, 'group', split_axis=0, concat_axis=0, tiled=T...  38.3 us
    gather x1, local copies, waits for them, and re-layouts, body(): outgoing = keys_padded[source].reshape(groups, capacity)  34.5 us
    reduce_scatter x1, waiting for transfers between devices, body(): lax.psum_scatter(q_part.astype(jnp.bfloat16), 'local', scatter_dimension=...  26.9 us
  transfers between devices with their start and end apart: 9, of which 8 were waited for; matrix products, arithmetic and copies ran while one was open for 24% of the time, Pallas kernels for 0%

profile of v1, /device:TPU:0, one launch (start us, length us, event | category | flops | bytes accessed | tf_op | source)
XLA Modules:
  0.0 679.7 jit_solution(4859317630325263572)
XLA Ops:
  11.3 12.8 %scatter_custom_fusion = s32[6656]{0:T(1024)S(1)} fusion(s32[3328]{0:T(1024)S(1)} %fusion.38, s32[3328]{0:T(1024)S(1)} %iota.29, s32[]{:T(128)} %constant.27.clone.1), kind=kCustom, calls=%fused_computation.84 | custom fusion | bytes 26628 | tf_op jit(solution)/shard_map/scatter | solution.py:117
  24.1 34.5 %gather_fusion = s32[6656]{0:T(1024)S(1)} fusion(s32[3329]{0:T(1024)S(1)} %pad_add_fusion, s32[7168]{0:T(1024)S(1)} %pad_clamp_fusion.1), kind=kCustom, calls=%fused_computation | custom fusion | bytes 79872 | tf_op jit(solution)/shard_map/gather | solution.py:121
  59.3 7.3 %all-to-all-start = ((s32[8,1,832]{2,1,0:T(1,128)}), s32[8,1,832]{2,1,0:T(1,128)S(1)}, u32[]{:S(2)}, u32[]{:S(2)}) async-start(s32[8,1,832]{2,1,0:T(1,128)} %all_to_all.14), calls=%async_computation | async-start | bytes 57344 | tf_op jit(solution)/shard_map/all_to_all | solution.py:123
  69.3 4.0 all-to-all-done
  73.5 14.3 %gather_fusion.1 = bf16[6656,128]{1,0:T(8,128)(2,1)} fusion(bf16[3328,128]{1,0:T(8,128)(2,1)S(1)} %reshape.127, s32[7168]{0:T(1024)S(1)} %pad_clamp_fusion), kind=kCustom, calls=%fused_computation.1 | custom fusion | bytes 3434496 | tf_op jit(solution)/shard_map/gather | solution.py:124
  87.7 3.7 all-to-all-start.1
  91.8 38.3 %all-to-all-done.1 = bf16[8,832,128]{2,1,0:T(8,128)(2,1)S(1)} async-done(((bf16[8,832,128]{2,1,0:T(8,128)(2,1)}), bf16[8,832,128]{2,1,0:T(8,128)(2,1)S(1)}, u32[]{:S(2)}, u32[]{:S(2)}) %all-to-all-start.1) | async-done | bytes 1703968 | tf_op jit(solution)/shard_map/all_to_all | solution.py:125
  130.1 6.5 gather_fusion.2
  137.4 7.3 %fusion.5 = (bf16[128,26,128]{2,0,1:T(8,128)(2,1)S(1)}, f32[26,128,128]{2,1,0:T(8,128)}) fusion(f32[128,26,128]{2,1,0:T(8,128)S(1)} %reshape.131, f32[256,26,128]{2,0,1:T(8,128)} %all-gather.3.cloned.1.call-done, s32[128,26]{0,1:T(8,128)S(1)} %copy-done.25), kind=kOutput, calls=%fused_computation.19 | convolution fusion | flops 1310326784 | bytes 7681024 | tf_op jit(solution)/shard_map/btr,rtd->btd/dot_general | solution.py:132
  146.5 4.9 gather_fusion.3
  159.2 19.0 %scatter_fusion = f32[128,27,27]{0,2,1:T(8,128)S(1)} fusion(f32[128,27,27]{0,2,1:T(8,128)S(1)} %broadcast_in_dim.21, s32[351]{0:T(512)S(1)} %copy-done, f32[351,128]{1,0:T(8,128)S(1)} %convolution_bitcast_fusion), kind=kCustom, calls=%fused_computation.6 | custom fusion | bytes 541944 | tf_op jit(solution)/shard_map/scatter | solution.py:33
  181.4 3.3 fusion.14
  184.7 6.2 fusion.4
  194.3 14.3 %gather_fusion.4 = bf16[6656,128]{1,0:T(8,128)(2,1)} fusion(bf16[3329,128]{1,0:T(8,128)(2,1)S(1)} %concatenate.24, s32[7168]{0:T(1024)S(1)} %pad_clamp_fusion.1), kind=kCustom, calls=%fused_computation.4 | custom fusion | bytes 3434496 | tf_op jit(solution)/shard_map/gather | solution.py:145
  208.6 3.6 all-to-all-start.2
  213.0 58.9 %all-to-all-done.2 = bf16[8,832,128]{2,1,0:T(8,128)(2,1)S(1)} async-done(((bf16[8,832,128]{2,1,0:T(8,128)(2,1)}), bf16[8,832,128]{2,1,0:T(8,128)(2,1)S(1)}, u32[]{:S(2)}, u32[]{:S(2)}) %all-to-all-start.2) | async-done | bytes 1703968 | tf_op jit(solution)/shard_map/all_to_all | solution.py:147
  271.9 39.3 %scatter_custom_fusion.2 = f32[3328,128]{1,0:T(8,128)S(1)} fusion(s32[6656]{0:T(1024)} %reshape.188, bf16[6656,128]{1,0:T(8,128)(2,1)S(1)} %bitcast.55, f32[]{:T(128)} %constant.24.clone.1), kind=kCustom, calls=%fused_computation.9 | custom fusion | flops 1703936 | bytes 3408384 | tf_op jit(solution)/shard_map/scatter-add | solution.py:154
  320.3 33.6 %all-reduce.7.cloned.1.call-done = f32[256,26,128]{0,2,1:T(8,128)} async-done(((f32[256,26,128]{0,2,1:T(8,128)}), f32[256,26,128]{0,2,1:T(8,128)}) %all-reduce.7.cloned.1.call-update) | async-done | bytes 3407888 | tf_op jit(solution)/shard_map/psum | solution.py:169
  353.9 26.9 %reduce-scatter.2.cloned.1.call-done = bf16[32,26,128]{2,1,0:T(8,128)(2,1)} async-done(((bf16[128,26,128]{2,1,0:T(8,128)(2,1)}), bf16[32,26,128]{2,1,0:T(8,128)(2,1)}) %reduce-scatter.2.cloned.1.call-update) | async-done | bytes 213008 | tf_op jit(solution)/shard_map/reduce_scatter | solution.py:157
  384.4 41.1 %all-reduce.1 = (f32[1024]{0:T(1024)S(1)}, f32[1024]{0:T(1024)S(1)}, f32[512]{0:T(512)S(1)}, f32[256]{0:T(256)S(1)}) all-reduce(f32[1024]{0:T(1024)S(1)} %get-tuple-element.50, f32[1024]{0:T(1024)S(1)} %get-tuple-element.52, f32[512]{0:T(512)} %get-tuple-element.54, ...), channel_id=1, replica_groups=mesh['group'=8,'local'=4] {'group','local'}, use_global_device_ids=true, to_apply=%region_10.11 | all-reduce | flops 2816 | bytes 22528 | tf_op jit(solution)/shard_map/psum | solution.py:174
  428.7 143.8 %all-reduce.11.cloned.1.call-done = (f32[479,1024]{1,0:T(8,128)}, f32[1024,1024]{1,0:T(8,128)}, f32[1024,512]{1,0:T(8,128)}, f32[512,256]{1,0:T(8,128)}) async-done(((f32[479,1024]{1,0:T(8,128)}, f32[1024,1024]{1,0:T(8,128)}, f32[1024,512]{1,0:T(8,128)}, f32[512,256]{1,0:T(8,128)}), (f32[479,1024]{1,0:T(8,128)}, f32[1024,1024]{1,0:T(8,128)}, f32[1024,512]{1,0:T(8,128)}, ...) | async-done | bytes 8777744 | tf_op jit(solution)/shard_map/psum | solution.py:174
  574.6 3.4 multiply_subtract_fusion.2
  584.2 63.3 %all-reduce.9.cloned.1.call-done = f32[256,26,128]{0,2,1:T(8,128)} async-done(((f32[256,26,128]{0,2,1:T(8,128)}), f32[256,26,128]{0,2,1:T(8,128)}) %all-reduce.9.cloned.1.call-update) | async-done | bytes 3407888 | tf_op jit(solution)/shard_map/psum | solution.py:169
  650.8 19.2 %all-gather.5.cloned.1.call-done = f32[128,26,128]{2,0,1:T(8,128)} async-done(((f32[32,26,128]{2,0,1:T(8,128)}), f32[128,26,128]{2,0,1:T(8,128)}) %all-gather.5.cloned.1.call-update) | async-done | bytes 1703952 | tf_op jit(solution)/shard_map/all_gather | solution.py:162
  (145 shorter events, 55.6 us)
Async XLA Ops:
  7.2 129.7 %all-gather.3.cloned.1.call-start = ((), (), s32[]{:S(2)}) async-start(), calls=%async_computation.4 | async-start | bytes 4259840 | tf_op jit(solution)/shard_map/all_gather | solution.py:127
  59.3 14.0 %all-to-all-start = ((s32[8,1,832]{2,1,0:T(1,128)}), s32[8,1,832]{2,1,0:T(1,128)S(1)}, u32[]{:S(2)}, u32[]{:S(2)}) async-start(s32[8,1,832]{2,1,0:T(1,128)} %all_to_all.14), calls=%async_computation | async-start | bytes 57344 | tf_op jit(solution)/shard_map/all_to_all | solution.py:123
  69.1 18.6 %copy-start.3 = (f32[128,26,128]{2,1,0:T(8,128)}, f32[128,26,128]{2,1,0:T(8,128)S(1)}, u32[]{:S(2)}) copy-start(f32[128,26,128]{2,1,0:T(8,128)S(1)} %copy.64) | copy-start | bytes 5111812
  87.7 4.0 copy-start.22
  87.7 42.4 %all-to-all-start.1 = ((bf16[8,832,128]{2,1,0:T(8,128)(2,1)}), bf16[8,832,128]{2,1,0:T(8,128)(2,1)S(1)}, u32[]{:S(2)}, u32[]{:S(2)}) async-start(bf16[8,832,128]{2,1,0:T(8,128)(2,1)} %bitcast.54), calls=%async_computation.1 | async-start | bytes 3407872 | tf_op jit(solution)/shard_map/all_to_all | solution.py:125
  91.5 262.4 %all-reduce.7.cloned.1.call-start = ((), (), s32[]{:S(2)}) async-start(), calls=%async_computation.7 | async-start | bytes 6815744 | tf_op jit(solution)/shard_map/psum | solution.py:169
  136.9 7.8 %copy-start.1 = (f32[128,26,128]{2,1,0:T(8,128)}, f32[128,26,128]{2,1,0:T(8,128)S(1)}, u32[]{:S(2)}) copy-start(f32[128,26,128]{2,1,0:T(8,128)S(1)} %reshape.131) | copy-start | bytes 5111812
  144.7 6.7 copy-start.5
  144.8 6.7 copy-start.28
  145.4 6.4 copy-start.29
  151.8 4.8 copy-start.10
  158.7 19.5 %copy-start.20 = (bf16[128,1024]{1,0:T(8,128)(2,1)}, bf16[128,1024]{1,0:T(8,128)(2,1)S(1)}, u32[]{:S(2)}) copy-start(bf16[128,1024]{1,0:T(8,128)(2,1)S(1)} %get-tuple-element.51) | copy-start | bytes 786436
  208.6 63.3 %all-to-all-start.2 = ((bf16[8,832,128]{2,1,0:T(8,128)(2,1)}), bf16[8,832,128]{2,1,0:T(8,128)(2,1)S(1)}, u32[]{:S(2)}, u32[]{:S(2)}) async-start(bf16[8,832,128]{2,1,0:T(8,128)(2,1)} %bitcast.10), calls=%async_computation.2 | async-start | bytes 3407872 | tf_op jit(solution)/shard_map/all_to_all | solution.py:147
  212.2 168.6 %reduce-scatter.2.cloned.1.call-start = ((), (), s32[]{:S(2)}) async-start(), calls=%async_computation.5 | async-start | bytes 1310720 | tf_op jit(solution)/shard_map/reduce_scatter | solution.py:157
  312.5 260.0 %all-reduce.11.cloned.1.call-start = ((), (), s32[]{:S(2)}) async-start(), calls=%async_computation.9 | async-start | bytes 17563648 | tf_op jit(solution)/shard_map/psum | solution.py:174
  313.9 3.5 copy-start.11
  313.9 3.5 copy-start.19
  320.2 327.3 %all-reduce.9.cloned.1.call-start = ((), (), s32[]{:S(2)}) async-start(), calls=%async_computation.8 | async-start | bytes 6815744 | tf_op jit(solution)/shard_map/psum | solution.py:169
  353.8 29.2 %copy-start.7 = (f32[64,26,128]{2,0,1:T(8,128)S(1)}, f32[64,26,128]{2,0,1:T(8,128)}, u32[]{:S(2)}) copy-start(f32[64,26,128]{2,0,1:T(8,128)} %param.25) | copy-start | bytes 2555908
  353.9 316.1 %all-gather.5.cloned.1.call-start = ((), (), s32[]{:S(2)}) async-start(), calls=%async_computation.6 | async-start | bytes 2129920 | tf_op jit(solution)/shard_map/all_gather | solution.py:162
  383.0 191.5 %copy-start.6 = (bf16[479,1024]{1,0:T(8,128)(2,1)S(1)}, bf16[479,1024]{1,0:T(8,128)(2,1)}, u32[]{:S(2)}) copy-start(bf16[479,1024]{1,0:T(8,128)(2,1)} %param.29) | copy-start | bytes 2942980
  572.5 5.5 copy-start.14
  574.6 5.1 copy-start.9
  578.0 3.4 copy-start.4
  (18 other events, 38.0 us)
Sparse Core Ops, SparseCore 0:
  9.5 32.7 all-gather.2
  191.1 162.7 all-reduce.6
  356.9 23.8 reduce-scatter.1
  387.5 184.9 all-reduce.10
  574.7 72.7 all-reduce.8
  649.5 20.4 all-gather.4
